TPU v7x, 32 devices: a whole 2x2x4 slice. The times are simulated.
32 devices in a mesh: groups: 2 (over y), blk: 16 (over z, x, core).
Axes of the slice: x: 2, y: 2, z: 4, core: 2. Of those that a mesh axis runs over, the one named last changes fastest.
Arguments:
- basis: float32 [8, 64, 480, 128], P(None, ('groups', 'blk')), parts along dimension 1
- nbr_block: int32 [64, 14], P(('groups', 'blk')), parts along dimension 0, may hold values from 0 to 31, as said below
- nbr_type: int32 [64, 14], P(('groups', 'blk')), parts along dimension 0, may hold values from 0 to 7
- nbr_count: int32 [64], P(('groups', 'blk')), parts along dimension 0, may hold values from 2 to 14, as said below
- sphere_type: int32 [64, 128], P(('groups', 'blk')), parts along dimension 0, may hold values from 0 to 3
- trans: float32 [8, 480, 480], replicated, may hold values from -0.25 to 0.25
- coup: float32 [8, 128, 128], replicated, may hold values from -0.5 to 0.5
- tmat: float32 [4, 480, 480], replicated, may hold values from -0.125 to 0.125
Outputs:
- new_vectors: float32 [2, 64, 480, 128], P(None, ('groups', 'blk')), parts along dimension 1
- hess_first: float32 [18], P('groups'), parts along dimension 0
- hess_second: float32 [20], P('groups'), parts along dimension 0
There are 2 independent parts, one for each index of `groups`. A program takes and returns all parts, laid end to end along the dimension named above; an argument that names none is the same for every part. Nothing has to cross between parts.
Inputs may be any that keep to these rules, and one draw needn't show every extreme that they name: `nbr_block`: each entry lies within 2 blocks of its own block; a block may be near itself. The first two slots of block b hold, in either order, the blocks b - 2 and b + 2, clipped to the cluster. Block b uses the first nbr_count[b] slots of its lists; some run of blocks uses all 14.
All inputs are finite; a program needn't handle non-finite values.
Results may differ from a plain program's by a relative error of at most 0.0003.
Values sent between devices are 32-bit elements; how exact they have to be, the bound alone decides.
A program may use at most 128 MiB of HBM per device.

v0:
```python
import functools

import jax
import jax.numpy as jnp
from jax import lax
from jax.experimental import pallas as pl
from jax.experimental.pallas import tpu as pltpu
from jax.sharding import PartitionSpec as P

F32 = jnp.float32
BF16 = jnp.bfloat16
REACH = 2
MESH = pl.DeviceIdType.MESH


def split(x):
    hi = x.astype(BF16)
    return hi, (x - hi.astype(F32)).astype(BF16)


def mm(a, b):
    return jnp.dot(a, b, preferred_element_type=F32)


def kernel(
    n, dims, w_ref, stype, basis, trans, coup, tmat, out, hess,
    bv, stage, mstage, cstage, thi, tlo, mhi, mlo, rct, halo1, halo2,
    za_hi, za_lo, zb_hi, zb_lo, acc, wbuf, fbuf, gbuf, send1, send2, slots1, slots2,
    lsem, ssem, rsem, hsend, hrecv, osem,
):
    kry, nb, coef, spb, kinds, skinds, cpad = dims
    window = 3 * nb
    me = lax.axis_index("blk")
    cells = float(n * nb * coef * spb)

    loads = [pltpu.make_async_copy(basis.at[kry - 1], bv.at[kry - 1], lsem.at[0])]
    loads.append(pltpu.make_async_copy(coup, cstage, lsem.at[1]))
    tl = [pltpu.make_async_copy(trans.at[t], stage.at[t], lsem.at[2 + t]) for t in range(kinds)]
    bl = pltpu.make_async_copy(
        basis.at[pl.ds(0, kry - 1)], bv.at[pl.ds(0, kry - 1)], lsem.at[2 + kinds]
    )
    ml_ = [
        pltpu.make_async_copy(tmat.at[t], mstage.at[t], lsem.at[3 + kinds + t])
        for t in range(skinds)
    ]
    for c in loads + tl + [bl] + ml_:
        c.start()

    barrier = pltpu.get_barrier_semaphore()

    def greet(d, _):
        pl.semaphore_signal(
            barrier, inc=1, device_id={"blk": lax.rem(me + d, n)}, device_id_type=MESH
        )
        return 0

    lax.fori_loop(1, n, greet, 0)
    pl.semaphore_wait(barrier, n - 1)

    def halo_copy(src, halo, step, side):
        peer = jnp.minimum(me + 1, n - 1) if side == 0 else jnp.maximum(me - 1, 0)
        return pltpu.make_async_remote_copy(
            src_ref=src,
            dst_ref=halo.at[side],
            send_sem=hsend.at[2 * step + side],
            recv_sem=hrecv.at[2 * step + side],
            device_id={"blk": peer},
            device_id_type=MESH,
        )

    def halo_start(src, halo, step):
        @pl.when(me < n - 1)
        def _():
            halo_copy(src, halo, step, 0).start()

        @pl.when(me > 0)
        def _():
            halo_copy(src, halo, step, 1).start()

    def halo_wait(src, halo, step):
        @pl.when(me < n - 1)
        def _():
            halo_copy(src, halo, step, 0).wait_send()
            halo_copy(src, halo, step, 1).wait_recv()

        @pl.when(me > 0)
        def _():
            halo_copy(src, halo, step, 1).wait_send()
            halo_copy(src, halo, step, 0).wait_recv()

    halo_start(basis.at[kry - 1], halo1, 0)

    @pl.when(me == 0)
    def _():
        halo1[0] = jnp.zeros(halo1.shape[1:], F32)
        halo2[0] = jnp.zeros(halo2.shape[1:], F32)

    @pl.when(me == n - 1)
    def _():
        halo1[1] = jnp.zeros(halo1.shape[1:], F32)
        halo2[1] = jnp.zeros(halo2.shape[1:], F32)

    tail = (coef // 128) * 128
    if cpad > coef:
        for z in (za_hi, za_lo, zb_hi, zb_lo):
            z[coef:, :] = jnp.zeros((cpad - coef, z.shape[1]), BF16)

    loads[1].wait()
    for t in range(kinds):
        ch, cl = split(cstage[t])
        rct[t, :spb, :spb] = ch
        rct[t, :spb, spb:] = ch
        rct[t, spb:, :spb] = cl
        rct[t, spb:, spb:] = cl

    def prepare(src, hi_ref, lo_ref, count):
        def one(t, _):
            hi, lo = split(src[t])
            if cpad > coef:
                hi_ref[t, :, tail:] = jnp.zeros((coef, cpad - tail), BF16)
                lo_ref[t, :, tail:] = jnp.zeros((coef, cpad - tail), BF16)
            hi_ref[t, :, :coef] = hi
            lo_ref[t, :, :coef] = lo
            return 0

        lax.fori_loop(0, count, one, 0)

    for c in tl:
        c.wait()
    prepare(stage, thi, tlo, kinds)
    loads[0].wait()
    bl.wait()

    pairs = [(i, j) for i in range(kry) for j in range(i, kry)]
    groups = coef // 8

    def sums(count, terms, b_count=nb):
        def row(r, carry):
            at = pl.ds(pl.multiple_of(r * 8, 8), 8)
            for b in range(b_count):
                new = terms(b, at)
                carry = tuple(x + y for x, y in zip(carry, new))
            return carry

        return lax.fori_loop(0, groups, row, (jnp.zeros((8, 128), F32),) * count)

    def gram_terms(b, at):
        vs = [bv[i, b, at, :] for i in range(kry)]
        return [vs[i] * vs[j] for i, j in pairs]

    gram = sums(len(pairs), gram_terms)
    gbuf[...] = jnp.concatenate(
        [jnp.sum(g, axis=0, keepdims=True) for g in gram]
        + [jnp.zeros((gbuf.shape[0] - len(pairs), 128), F32)],
        axis=0,
    )
    for c in ml_:
        c.wait()
    prepare(mstage, mhi, mlo, skinds)

    def operator_apply(vec, halo):
        def source(p):
            if p < nb:
                return halo[0, p]
            if p < 2 * nb:
                return vec[p - nb]
            return halo[1, p - 2 * nb]

        def couple(t, hi_ref, lo_ref):
            for b in range(nb):
                m = None
                for p in range(nb + b - REACH, nb + b + REACH + 1):
                    term = w_ref[(b * kinds + t) * window + p] * source(p)
                    m = term if m is None else m + term
                mh, ml = split(m)
                r = lax.dot_general(
                    jnp.concatenate([mh, ml], axis=1),
                    rct[t],
                    (((1,), (1,)), ((), ())),
                    preferred_element_type=F32,
                )
                zh, zl = split(r[:, :spb] + r[:, spb:])
                hi_ref[:coef, b * spb : (b + 1) * spb] = zh
                lo_ref[:coef, b * spb : (b + 1) * spb] = zl

        def move(t, hi_ref, lo_ref):
            hi = hi_ref[...]
            acc[...] += mm(thi[t], hi) + mm(thi[t], lo_ref[...]) + mm(tlo[t], hi)

        acc[...] = jnp.zeros(acc.shape, F32)
        couple(0, za_hi, za_lo)

        def two(u, _):
            move(2 * u, za_hi, za_lo)
            couple(2 * u + 1, zb_hi, zb_lo)
            move(2 * u + 1, zb_hi, zb_lo)
            couple(jnp.minimum(2 * u + 2, kinds - 1), za_hi, za_lo)
            return 0

        lax.fori_loop(0, kinds // 2, two, 0)
        sh, sl = split(acc[...])
        za_hi[:coef, :] = sh
        za_lo[:coef, :] = sl
        acc[...] = jnp.concatenate([vec[b] for b in range(nb)], axis=1)
        kind_row = jnp.concatenate([stype[b : b + 1, :] for b in range(nb)], axis=1)

        def scatter(t, _):
            hi = za_hi[...]
            y = mm(mhi[t], hi) + mm(mhi[t], za_lo[...]) + mm(mlo[t], hi)
            mask = (kind_row == t).astype(F32)
            acc[...] -= mask * y
            return 0

        lax.fori_loop(0, skinds, scatter, 0)
        for b in range(nb):
            wbuf[b] = acc[:, b * spb : (b + 1) * spb]

    lane = lax.broadcasted_iota(jnp.int32, (8, 128), 1)

    def allreduce(step, rows, send, slots):
        k = rows.shape[0]
        tot = jnp.sum(rows, axis=1, keepdims=True)
        here = lax.broadcasted_iota(jnp.int32, (k, 128), 1) == lax.broadcasted_iota(
            jnp.int32, (k, 128), 0
        )
        packed = jnp.sum(jnp.where(here, tot, 0.0), axis=0, keepdims=True)
        packed = jnp.broadcast_to(packed, (8, 128))
        send[...] = packed
        slots[me] = packed

        def copy(d, slot, peer):
            return pltpu.make_async_remote_copy(
                src_ref=send,
                dst_ref=slots.at[slot],
                send_sem=ssem.at[step, d],
                recv_sem=rsem.at[step, slot],
                device_id={"blk": peer},
                device_id_type=MESH,
            )

        def go(d, _):
            copy(d, me, lax.rem(me + d, n)).start()
            return 0

        def done(d, _):
            peer = lax.rem(me + d, n)
            c = copy(d, peer, peer)
            c.wait_send()
            c.wait_recv()
            return 0

        lax.fori_loop(1, n, go, 0)
        lax.fori_loop(1, n, done, 0)
        total = jnp.sum(slots[...], axis=0)
        return lambda i: jnp.sum(jnp.where(lane == i, total, 0.0), axis=1, keepdims=True)

    def pack(parts, more):
        rows = [jnp.sum(x, axis=0, keepdims=True) for x in parts]
        pad = (-len(rows)) % 8
        rows += [jnp.zeros((1, 128), F32)] * pad
        head = jnp.concatenate(rows, axis=0)
        return (head if more is None else jnp.concatenate([head, more], axis=0)), len(rows)

    def norm(count, proj, image_sq, gram_of):
        coeffs = [x / cells for x in proj]
        squares = image_sq
        for i in range(count):
            inner = None
            for j in range(count):
                term = gram_of(i, j) * coeffs[j]
                inner = term if inner is None else inner + term
            squares = squares + coeffs[i] * (inner - 2.0 * proj[i])
        return coeffs, jnp.sqrt(squares / cells + 1e-06)

    def hess_row(coeffs, beta):
        row = jnp.zeros((8, 128), F32)
        for i, c in enumerate(coeffs + [beta]):
            row = jnp.where(lane == i, c, row)
        return row

    halo_wait(basis.at[kry - 1], halo1, 0)
    operator_apply(bv.at[kry - 1], halo1)

    def proj_terms1(b, at):
        w = wbuf[b, at, :]
        return [w * bv[i, b, at, :] for i in range(kry)] + [w * w]

    rows, base = pack(sums(kry + 1, proj_terms1), gbuf[...])
    get1 = allreduce(0, rows, send1, slots1)
    gram8 = {}
    for k, (i, j) in enumerate(pairs):
        gram8[i, j] = gram8[j, i] = get1(base + k)
    h1, beta1 = norm(kry, [get1(i) for i in range(kry)], get1(kry), lambda i, j: gram8[i, j])
    hess[0] = hess_row(h1, beta1)
    inv1 = 1.0 / beta1

    def first_terms(b, at):
        f = wbuf[b, at, :]
        vs = [bv[i, b, at, :] for i in range(kry)]
        for i in range(kry):
            f = f - h1[i] * vs[i]
        f = f * inv1
        fbuf[0, b, at, :] = f
        return [f * v for v in vs] + [f * f]

    extra = sums(kry + 1, first_terms)
    halo_start(fbuf.at[0], halo2, 1)
    first_out = pltpu.make_async_copy(fbuf.at[0], out.at[0], osem.at[0])
    first_out.start()

    halo_wait(fbuf.at[0], halo2, 1)
    operator_apply(fbuf.at[0], halo2)

    def proj_terms2(b, at):
        w = wbuf[b, at, :]
        return [w * bv[i, b, at, :] for i in range(kry)] + [w * fbuf[0, b, at, :], w * w]

    rows, _ = pack(tuple(sums(kry + 2, proj_terms2)) + tuple(extra), None)
    get2 = allreduce(1, rows, send2, slots2)
    gram9 = dict(gram8)
    for i in range(kry + 1):
        gram9[i, kry] = gram9[kry, i] = get2(kry + 2 + i)
    h2, beta2 = norm(
        kry + 1, [get2(i) for i in range(kry + 1)], get2(kry + 1), lambda i, j: gram9[i, j]
    )
    hess[1] = hess_row(h2, beta2)
    inv2 = 1.0 / beta2

    def second(r, _):
        at = pl.ds(pl.multiple_of(r * 8, 8), 8)
        for b in range(nb):
            f = wbuf[b, at, :]
            for i in range(kry):
                f = f - h2[i] * bv[i, b, at, :]
            f = f - h2[kry] * fbuf[0, b, at, :]
            fbuf[1, b, at, :] = f * inv2
        return 0

    lax.fori_loop(0, groups, second, 0)
    second_out = pltpu.make_async_copy(fbuf.at[1], out.at[1], osem.at[1])
    second_out.start()
    first_out.wait()
    second_out.wait()


def shards(n, basis, nbr_block, nbr_type, nbr_count, sphere_type, trans, coup, tmat):
    kry, nb, coef, spb = basis.shape
    kinds, skinds = trans.shape[0], tmat.shape[0]
    cpad = -(-coef // 128) * 128
    window = 3 * nb
    rows = nbr_block - lax.axis_index("blk") * nb + nb
    live = jnp.arange(nbr_block.shape[1], dtype=jnp.int32)[None, :] < nbr_count[:, None]
    code = jnp.where(live, nbr_type * window + rows, -1)
    weights = jnp.sum(
        (code[:, None, :] == jnp.arange(kinds * window, dtype=jnp.int32)[None, :, None]).astype(F32),
        axis=2,
    ).reshape(-1)
    npairs = kry * (kry + 1) // 2
    any_ = pl.BlockSpec(memory_space=pl.ANY)
    vm = pl.BlockSpec(memory_space=pltpu.VMEM)
    wide = nb * spb
    out, hess = pl.pallas_call(
        functools.partial(kernel, n, (kry, nb, coef, spb, kinds, skinds, cpad)),
        out_shape=(
            jax.ShapeDtypeStruct((2, nb, coef, spb), F32),
            jax.ShapeDtypeStruct((2, 8, 128), F32),
        ),
        in_specs=[pl.BlockSpec(memory_space=pltpu.SMEM), vm, any_, any_, any_, any_],
        out_specs=(any_, vm),
        scratch_shapes=[
            pltpu.VMEM((kry, nb, coef, spb), F32),
            pltpu.VMEM((kinds, coef, coef), F32),
            pltpu.VMEM((skinds, coef, coef), F32),
            pltpu.VMEM((kinds, spb, spb), F32),
            pltpu.VMEM((kinds, coef, cpad), BF16),
            pltpu.VMEM((kinds, coef, cpad), BF16),
            pltpu.VMEM((skinds, coef, cpad), BF16),
            pltpu.VMEM((skinds, coef, cpad), BF16),
            pltpu.VMEM((kinds, 2 * spb, 2 * spb), BF16),
            pltpu.VMEM((2, nb, coef, spb), F32),
            pltpu.VMEM((2, nb, coef, spb), F32),
        ]
        + [pltpu.VMEM((cpad, wide), BF16)] * 4
        + [
            pltpu.VMEM((coef, wide), F32),
            pltpu.VMEM((nb, coef, spb), F32),
            pltpu.VMEM((2, nb, coef, spb), F32),
            pltpu.VMEM((-(-npairs // 8) * 8, 128), F32),
            pltpu.VMEM((8, 128), F32),
            pltpu.VMEM((8, 128), F32),
            pltpu.VMEM((n, 8, 128), F32),
            pltpu.VMEM((n, 8, 128), F32),
            pltpu.SemaphoreType.DMA((3 + kinds + skinds,)),
            pltpu.SemaphoreType.DMA((2, n)),
            pltpu.SemaphoreType.DMA((2, n)),
            pltpu.SemaphoreType.DMA((4,)),
            pltpu.SemaphoreType.DMA((4,)),
            pltpu.SemaphoreType.DMA((2,)),
        ],
        compiler_params=pltpu.CompilerParams(
            collective_id=0, has_side_effects=True, vmem_limit_bytes=60 * 1024 * 1024
        ),
    )(weights, sphere_type, basis, trans, coup, tmat)
    return out, hess[0, 0, : kry + 1], hess[1, 0, : kry + 2]


def solution(mesh):
    return jax.shard_map(
        functools.partial(shards, mesh.shape["blk"]),
        mesh=mesh,
        in_specs=(
            P(None, ("groups", "blk"), None, None),
            P(("groups", "blk"), None),
            P(("groups", "blk"), None),
            P(("groups", "blk")),
            P(("groups", "blk"), None),
            P(),
            P(),
            P(),
        ),
        out_specs=(P(None, ("groups", "blk"), None, None), P("groups"), P("groups")),
        check_vma=False,
    )
```

profile of v0, /device:TPU:0, one launch (start us, length us, event | category | flops | bytes accessed | tf_op | source)
XLA Modules:
  0.0 72.4 jit_solution(16445325069741494253)
XLA Ops:
  0.6 0.8 %compare_select_fusion = s32[2,14]{1,0:T(2,128)S(1)} fusion(s32[2,14]{1,0:T(2,128)} %param.9, s32[2,14]{1,0:T(2,128)} %param.10, s32[]{:T(128)S(6)} %mul.7, s32[2]{0:T(128)} %param.11), kind=kLoop, calls=%fused_computation.2 | loop fusion | flops 168 | bytes 348 | tf_op jit(solution)/shard_map/jit(_where)/select_n | solution.py:353
  1.4 0.1 copy.11
  1.5 0.1 fusion
  1.6 0.6 reshape.11.w_ref
  2.2 65.7 %shard_map.103 = (f32[2,2,480,128]{3,2,1,0:T(8,128)}, f32[2,8,128]{2,1,0:T(8,128)}) custom-call(f32[96]{0:T(128)} %reshape.11.w_ref, s32[2,128]{1,0:T(2,128)} %stype.1, f32[8,2,480,128]{3,2,1,0:T(8,128)} %basis.1, f32[8,480,480]{2,1,0:T(8,128)} %trans.1, f32[8,128,128]{2,1,0:T(8,128)} %coup.1, f32[4,480,480]{2,1,0:T(8,128)} %tmat.1), custom_call_target="tpu_custom_call" | custom-call | tf_op jit(solution)/shard_map/pallas_call | solution.py:362
  67.9 1.2 %slice_bitcast_fusion = f32[10]{0:T(128)} fusion(f32[2,8,128]{2,1,0:T(8,128)} %get-tuple-element.6), kind=kLoop, calls=%fused_computation.3 | loop fusion | bytes 80 | tf_op jit(solution)/shard_map/squeeze | solution.py:404
  69.0 1.2 %slice_bitcast_fusion.1 = f32[9]{0:T(128)} fusion(f32[2,8,128]{2,1,0:T(8,128)} %get-tuple-element.6), kind=kLoop, calls=%fused_computation.4 | loop fusion | bytes 72 | tf_op jit(solution)/shard_map/squeeze | solution.py:404
  70.2 2.2 %copy.13 = f32[2,2,480,128]{3,2,1,0:T(8,128)} copy(f32[2,2,480,128]{3,2,1,0:T(8,128)} %get-tuple-element.10) | data formatting | bytes 1966080
where the time goes:
time: 72.7 us; the launch traced here: 72.4 us
  Pallas kernels  65.7 us (90%)
  local copies, waits for them, and re-layouts  5.27 us (7%)
  other arithmetic  0.86 us (1%)
    pallas_call x1, Pallas kernels, shards(): pl.pallas_call(functools.partial(kernel, n, (kry, nb, coef, spb, kinds, s...  65.7 us
    squeeze x2, local copies, waits for them, and re-layouts, shards(): return (out, hess[0, 0, :kry + 1], hess[1, 0, :kry + 2])  2.37 us
    unnamed x1, local copies, waits for them, and re-layouts  2.21 us

commit v1 on v0

--- a/solution.py
+++ b/solution.py
@@ -10,6 +10,7 @@
 F32 = jnp.float32
 BF16 = jnp.bfloat16
 REACH = 2
+CHUNK = 128
 MESH = pl.DeviceIdType.MESH
 
 
@@ -18,6 +19,11 @@
     return hi, (x - hi.astype(F32)).astype(BF16)
 
 
+def factors(n):
+    near = max(f for f in range(1, n + 1) if n % f == 0 and f * f <= n)
+    return near, n // near
+
+
 def mm(a, b):
     return jnp.dot(a, b, preferred_element_type=F32)
 
@@ -25,13 +31,22 @@
 def kernel(
     n, dims, w_ref, stype, basis, trans, coup, tmat, out, hess,
     bv, stage, mstage, cstage, thi, tlo, mhi, mlo, rct, halo1, halo2,
-    za_hi, za_lo, zb_hi, zb_lo, acc, wbuf, fbuf, gbuf, send1, send2, slots1, slots2,
-    lsem, ssem, rsem, hsend, hrecv, osem,
+    za_hi, za_lo, zb_hi, zb_lo, sh_ref, sl_ref, acc, wbuf, fbuf, gbuf,
+    send, slots_a, slots_b, lsem, ssem, ra_sem, rb_sem, hsend, hrecv, osem,
 ):
     kry, nb, coef, spb, kinds, skinds, cpad = dims
     window = 3 * nb
     me = lax.axis_index("blk")
     cells = float(n * nb * coef * spb)
+    near, far = factors(n)
+    chunks = [(c, min(CHUNK, coef - c)) for c in range(0, coef, CHUNK)]
+    my_far, my_near = lax.div(me, near), lax.rem(me, near)
+
+    def near_peer(d):
+        return my_far * near + lax.rem(my_near + d, near)
+
+    def far_peer(d):
+        return lax.rem(my_far + d, far) * near + my_near
 
     loads = [pltpu.make_async_copy(basis.at[kry - 1], bv.at[kry - 1], lsem.at[0])]
     loads.append(pltpu.make_async_copy(coup, cstage, lsem.at[1]))
@@ -48,47 +63,47 @@
 
     barrier = pltpu.get_barrier_semaphore()
 
-    def greet(d, _):
-        pl.semaphore_signal(
-            barrier, inc=1, device_id={"blk": lax.rem(me + d, n)}, device_id_type=MESH
-        )
-        return 0
-
-    lax.fori_loop(1, n, greet, 0)
-    pl.semaphore_wait(barrier, n - 1)
-
-    def halo_copy(src, halo, step, side):
+    partners = [lax.rem(me + 1, n), lax.rem(me + n - 1, n)]
+    partners += [near_peer(d) for d in range(1, near)]
+    partners += [far_peer(d) for d in range(1, far)]
+    for peer in partners:
+        pl.semaphore_signal(barrier, inc=1, device_id={"blk": peer}, device_id_type=MESH)
+    pl.semaphore_wait(barrier, len(partners))
+
+    def halo_copy(src, halo, step, side, c):
         peer = jnp.minimum(me + 1, n - 1) if side == 0 else jnp.maximum(me - 1, 0)
+        at = pl.ds(chunks[c][0], chunks[c][1])
         return pltpu.make_async_remote_copy(
-            src_ref=src,
-            dst_ref=halo.at[side],
-            send_sem=hsend.at[2 * step + side],
-            recv_sem=hrecv.at[2 * step + side],
+            src_ref=src.at[:, at, :],
+            dst_ref=halo.at[side, :, at, :],
+            send_sem=hsend.at[step, side, c],
+            recv_sem=hrecv.at[step, side, c],
             device_id={"blk": peer},
             device_id_type=MESH,
         )
 
-    def halo_start(src, halo, step):
+    def halo_start(src, halo, step, c):
         @pl.when(me < n - 1)
         def _():
-            halo_copy(src, halo, step, 0).start()
+            halo_copy(src, halo, step, 0, c).start()
 
         @pl.when(me > 0)
         def _():
-            halo_copy(src, halo, step, 1).start()
-
-    def halo_wait(src, halo, step):
+            halo_copy(src, halo, step, 1, c).start()
+
+    def halo_wait(src, halo, step, c):
         @pl.when(me < n - 1)
         def _():
-            halo_copy(src, halo, step, 0).wait_send()
-            halo_copy(src, halo, step, 1).wait_recv()
+            halo_copy(src, halo, step, 0, c).wait_send()
+            halo_copy(src, halo, step, 1, c).wait_recv()
 
         @pl.when(me > 0)
         def _():
-            halo_copy(src, halo, step, 1).wait_send()
-            halo_copy(src, halo, step, 0).wait_recv()
-
-    halo_start(basis.at[kry - 1], halo1, 0)
+            halo_copy(src, halo, step, 1, c).wait_send()
+            halo_copy(src, halo, step, 0, c).wait_recv()
+
+    for c in range(len(chunks)):
+        halo_start(basis.at[kry - 1], halo1, 0, c)
 
     @pl.when(me == 0)
     def _():
@@ -101,8 +116,10 @@
         halo2[1] = jnp.zeros(halo2.shape[1:], F32)
 
     tail = (coef // 128) * 128
+    for z in (za_hi, za_lo, zb_hi, zb_lo):
+        z[...] = jnp.zeros(z.shape, BF16)
     if cpad > coef:
-        for z in (za_hi, za_lo, zb_hi, zb_lo):
+        for z in (sh_ref, sl_ref):
             z[coef:, :] = jnp.zeros((cpad - coef, z.shape[1]), BF16)
 
     loads[1].wait()
@@ -127,22 +144,34 @@
 
     for c in tl:
         c.wait()
-    prepare(stage, thi, tlo, kinds)
+
+    def prepare_pair(u, _):
+        for k in range(2):
+            for dst, part in zip((thi, tlo), split(stage[2 * u + k])):
+                for c, (at, size) in enumerate(chunks):
+                    if size < CHUNK:
+                        dst[c, u, :, k * CHUNK : (k + 1) * CHUNK] = jnp.zeros((coef, CHUNK), BF16)
+                    dst[c, u, :, k * CHUNK : k * CHUNK + size] = part[:, at : at + size]
+        return 0
+
+    lax.fori_loop(0, kinds // 2, prepare_pair, 0)
     loads[0].wait()
     bl.wait()
 
     pairs = [(i, j) for i in range(kry) for j in range(i, kry)]
     groups = coef // 8
 
-    def sums(count, terms, b_count=nb):
+    def sums(count, terms, start=0, size=coef, carry=None):
         def row(r, carry):
             at = pl.ds(pl.multiple_of(r * 8, 8), 8)
-            for b in range(b_count):
+            for b in range(nb):
                 new = terms(b, at)
                 carry = tuple(x + y for x, y in zip(carry, new))
             return carry
 
-        return lax.fori_loop(0, groups, row, (jnp.zeros((8, 128), F32),) * count)
+        if carry is None:
+            carry = (jnp.zeros((8, 128), F32),) * count
+        return lax.fori_loop(start // 8, (start + size) // 8, row, carry)
 
     def gram_terms(b, at):
         vs = [bv[i, b, at, :] for i in range(kry)]
@@ -158,55 +187,65 @@
         c.wait()
     prepare(mstage, mhi, mlo, skinds)
 
-    def operator_apply(vec, halo):
-        def source(p):
+    def operator_apply(vec, sent, halo, step):
+        def source(p, at, size):
+            rows = slice(at, at + size)
             if p < nb:
-                return halo[0, p]
+                return halo[0, p, rows]
             if p < 2 * nb:
-                return vec[p - nb]
-            return halo[1, p - 2 * nb]
-
-        def couple(t, hi_ref, lo_ref):
-            for b in range(nb):
-                m = None
-                for p in range(nb + b - REACH, nb + b + REACH + 1):
-                    term = w_ref[(b * kinds + t) * window + p] * source(p)
-                    m = term if m is None else m + term
-                mh, ml = split(m)
+                return vec[p - nb, rows]
+            return halo[1, p - 2 * nb, rows]
+
+        def couple(c, u, hi_ref, lo_ref):
+            at, size = chunks[c]
+            for k in range(2):
+                t = 2 * u + k
+                parts = []
+                for b in range(nb):
+                    m = None
+                    for p in range(nb + b - REACH, nb + b + REACH + 1):
+                        term = w_ref[(b * kinds + t) * window + p] * source(p, at, size)
+                        m = term if m is None else m + term
+                    parts.append(jnp.concatenate(split(m), axis=1))
                 r = lax.dot_general(
-                    jnp.concatenate([mh, ml], axis=1),
+                    jnp.concatenate(parts, axis=0),
                     rct[t],
                     (((1,), (1,)), ((), ())),
                     preferred_element_type=F32,
                 )
                 zh, zl = split(r[:, :spb] + r[:, spb:])
-                hi_ref[:coef, b * spb : (b + 1) * spb] = zh
-                lo_ref[:coef, b * spb : (b + 1) * spb] = zl
-
-        def move(t, hi_ref, lo_ref):
+                for b in range(nb):
+                    to = (slice(k * CHUNK, k * CHUNK + size), slice(b * spb, (b + 1) * spb))
+                    hi_ref[to] = zh[b * size : (b + 1) * size]
+                    lo_ref[to] = zl[b * size : (b + 1) * size]
+
+        def move(c, u, hi_ref, lo_ref):
             hi = hi_ref[...]
-            acc[...] += mm(thi[t], hi) + mm(thi[t], lo_ref[...]) + mm(tlo[t], hi)
-
-        acc[...] = jnp.zeros(acc.shape, F32)
-        couple(0, za_hi, za_lo)
-
-        def two(u, _):
-            move(2 * u, za_hi, za_lo)
-            couple(2 * u + 1, zb_hi, zb_lo)
-            move(2 * u + 1, zb_hi, zb_lo)
-            couple(jnp.minimum(2 * u + 2, kinds - 1), za_hi, za_lo)
-            return 0
-
-        lax.fori_loop(0, kinds // 2, two, 0)
+            y = mm(thi[c, u], hi) + mm(thi[c, u], lo_ref[...]) + mm(tlo[c, u], hi)
+            if c == 0 and u == 0:
+                acc[...] = y
+            else:
+                acc[...] += y
+
+        bufs = ((za_hi, za_lo), (zb_hi, zb_lo))
+        turn = 0
+        for c in range(len(chunks)):
+            halo_wait(sent, halo, step, c)
+            couple(c, 0, *bufs[turn])
+            for u in range(kinds // 2):
+                if u + 1 < kinds // 2:
+                    couple(c, u + 1, *bufs[1 - turn])
+                move(c, u, *bufs[turn])
+                turn = 1 - turn
         sh, sl = split(acc[...])
-        za_hi[:coef, :] = sh
-        za_lo[:coef, :] = sl
+        sh_ref[:coef, :] = sh
+        sl_ref[:coef, :] = sl
         acc[...] = jnp.concatenate([vec[b] for b in range(nb)], axis=1)
         kind_row = jnp.concatenate([stype[b : b + 1, :] for b in range(nb)], axis=1)
 
         def scatter(t, _):
-            hi = za_hi[...]
-            y = mm(mhi[t], hi) + mm(mhi[t], za_lo[...]) + mm(mlo[t], hi)
+            hi = sh_ref[...]
+            y = mm(mhi[t], hi) + mm(mhi[t], sl_ref[...]) + mm(mlo[t], hi)
             mask = (kind_row == t).astype(F32)
             acc[...] -= mask * y
             return 0
@@ -217,7 +256,7 @@
 
     lane = lax.broadcasted_iota(jnp.int32, (8, 128), 1)
 
-    def allreduce(step, rows, send, slots):
+    def allreduce(step, rows):
         k = rows.shape[0]
         tot = jnp.sum(rows, axis=1, keepdims=True)
         here = lax.broadcasted_iota(jnp.int32, (k, 128), 1) == lax.broadcasted_iota(
@@ -225,33 +264,33 @@
         )
         packed = jnp.sum(jnp.where(here, tot, 0.0), axis=0, keepdims=True)
         packed = jnp.broadcast_to(packed, (8, 128))
-        send[...] = packed
-        slots[me] = packed
-
-        def copy(d, slot, peer):
-            return pltpu.make_async_remote_copy(
-                src_ref=send,
-                dst_ref=slots.at[slot],
-                send_sem=ssem.at[step, d],
-                recv_sem=rsem.at[step, slot],
-                device_id={"blk": peer},
-                device_id_type=MESH,
+        total = packed
+        for turn, (slots, rs, size, spot, peer_of) in enumerate(
+            (
+                (slots_a, ra_sem, near, my_near, near_peer),
+                (slots_b, rb_sem, far, my_far, far_peer),
             )
-
-        def go(d, _):
-            copy(d, me, lax.rem(me + d, n)).start()
-            return 0
-
-        def done(d, _):
-            peer = lax.rem(me + d, n)
-            c = copy(d, peer, peer)
-            c.wait_send()
-            c.wait_recv()
-            return 0
-
-        lax.fori_loop(1, n, go, 0)
-        lax.fori_loop(1, n, done, 0)
-        total = jnp.sum(slots[...], axis=0)
+        ):
+            send[step, turn] = total
+            slots[step, spot] = total
+
+            def copy(d, slot):
+                return pltpu.make_async_remote_copy(
+                    src_ref=send.at[step, turn],
+                    dst_ref=slots.at[step, slot],
+                    send_sem=ssem.at[step, turn, d],
+                    recv_sem=rs.at[step, slot],
+                    device_id={"blk": peer_of(d)},
+                    device_id_type=MESH,
+                )
+
+            for d in range(1, size):
+                copy(d, spot).start()
+            for d in range(1, size):
+                c = copy(d, lax.rem(spot + d, size))
+                c.wait_send()
+                c.wait_recv()
+            total = jnp.sum(slots[step], axis=0)
         return lambda i: jnp.sum(jnp.where(lane == i, total, 0.0), axis=1, keepdims=True)
 
     def pack(parts, more):
@@ -278,15 +317,14 @@
             row = jnp.where(lane == i, c, row)
         return row
 
-    halo_wait(basis.at[kry - 1], halo1, 0)
-    operator_apply(bv.at[kry - 1], halo1)
+    operator_apply(bv.at[kry - 1], basis.at[kry - 1], halo1, 0)
 
     def proj_terms1(b, at):
         w = wbuf[b, at, :]
         return [w * bv[i, b, at, :] for i in range(kry)] + [w * w]
 
     rows, base = pack(sums(kry + 1, proj_terms1), gbuf[...])
-    get1 = allreduce(0, rows, send1, slots1)
+    get1 = allreduce(0, rows)
     gram8 = {}
     for k, (i, j) in enumerate(pairs):
         gram8[i, j] = gram8[j, i] = get1(base + k)
@@ -303,20 +341,21 @@
         fbuf[0, b, at, :] = f
         return [f * v for v in vs] + [f * f]
 
-    extra = sums(kry + 1, first_terms)
-    halo_start(fbuf.at[0], halo2, 1)
+    extra = None
+    for c, (at, size) in enumerate(chunks):
+        extra = sums(kry + 1, first_terms, at, size, extra)
+        halo_start(fbuf.at[0], halo2, 1, c)
     first_out = pltpu.make_async_copy(fbuf.at[0], out.at[0], osem.at[0])
     first_out.start()
 
-    halo_wait(fbuf.at[0], halo2, 1)
-    operator_apply(fbuf.at[0], halo2)
+    operator_apply(fbuf.at[0], fbuf.at[0], halo2, 1)
 
     def proj_terms2(b, at):
         w = wbuf[b, at, :]
         return [w * bv[i, b, at, :] for i in range(kry)] + [w * fbuf[0, b, at, :], w * w]
 
     rows, _ = pack(tuple(sums(kry + 2, proj_terms2)) + tuple(extra), None)
-    get2 = allreduce(1, rows, send2, slots2)
+    get2 = allreduce(1, rows)
     gram9 = dict(gram8)
     for i in range(kry + 1):
         gram9[i, kry] = gram9[kry, i] = get2(kry + 2 + i)
@@ -359,6 +398,8 @@
     any_ = pl.BlockSpec(memory_space=pl.ANY)
     vm = pl.BlockSpec(memory_space=pltpu.VMEM)
     wide = nb * spb
+    nch = -(-coef // CHUNK)
+    near, far = factors(n)
     out, hess = pl.pallas_call(
         functools.partial(kernel, n, (kry, nb, coef, spb, kinds, skinds, cpad)),
         out_shape=(
@@ -372,29 +413,30 @@
             pltpu.VMEM((kinds, coef, coef), F32),
             pltpu.VMEM((skinds, coef, coef), F32),
             pltpu.VMEM((kinds, spb, spb), F32),
-            pltpu.VMEM((kinds, coef, cpad), BF16),
-            pltpu.VMEM((kinds, coef, cpad), BF16),
+            pltpu.VMEM((nch, kinds // 2, coef, 2 * CHUNK), BF16),
+            pltpu.VMEM((nch, kinds // 2, coef, 2 * CHUNK), BF16),
             pltpu.VMEM((skinds, coef, cpad), BF16),
             pltpu.VMEM((skinds, coef, cpad), BF16),
             pltpu.VMEM((kinds, 2 * spb, 2 * spb), BF16),
             pltpu.VMEM((2, nb, coef, spb), F32),
             pltpu.VMEM((2, nb, coef, spb), F32),
         ]
-        + [pltpu.VMEM((cpad, wide), BF16)] * 4
+        + [pltpu.VMEM((2 * CHUNK, wide), BF16)] * 4
+        + [pltpu.VMEM((cpad, wide), BF16)] * 2
         + [
             pltpu.VMEM((coef, wide), F32),
             pltpu.VMEM((nb, coef, spb), F32),
             pltpu.VMEM((2, nb, coef, spb), F32),
             pltpu.VMEM((-(-npairs // 8) * 8, 128), F32),
-            pltpu.VMEM((8, 128), F32),
-            pltpu.VMEM((8, 128), F32),
-            pltpu.VMEM((n, 8, 128), F32),
-            pltpu.VMEM((n, 8, 128), F32),
+            pltpu.VMEM((2, 2, 8, 128), F32),
+            pltpu.VMEM((2, near, 8, 128), F32),
+            pltpu.VMEM((2, far, 8, 128), F32),
             pltpu.SemaphoreType.DMA((3 + kinds + skinds,)),
-            pltpu.SemaphoreType.DMA((2, n)),
-            pltpu.SemaphoreType.DMA((2, n)),
-            pltpu.SemaphoreType.DMA((4,)),
-            pltpu.SemaphoreType.DMA((4,)),
+            pltpu.SemaphoreType.DMA((2, 2, max(near, far))),
+            pltpu.SemaphoreType.DMA((2, near)),
+            pltpu.SemaphoreType.DMA((2, far)),
+            pltpu.SemaphoreType.DMA((2, 2, nch)),
+            pltpu.SemaphoreType.DMA((2, 2, nch)),
             pltpu.SemaphoreType.DMA((2,)),
         ],
         compiler_params=pltpu.CompilerParams(

time: 72.7 us -> 65.5 us (0.901)
  Pallas kernels: 65.7 us -> 58.4 us
    pallas_call x1, Pallas kernels: 65.7 us -> 58.4 us  [shards(): pl.pallas_call(functools.partial(kernel, n, (kry, nb, coef, spb, kinds, s...]
where the time goes in v1:
time: 65.5 us; the launch traced here: 65.2 us
  Pallas kernels  58.4 us (89%)
  local copies, waits for them, and re-layouts  5.27 us (8%)
  other arithmetic  0.86 us (1%)
    pallas_call x1, Pallas kernels, shards(): pl.pallas_call(functools.partial(kernel, n, (kry, nb, coef, spb, kinds, s...  58.4 us
    squeeze x2, local copies, waits for them, and re-layouts, shards(): return (out, hess[0, 0, :kry + 1], hess[1, 0, :kry + 2])  2.37 us
    unnamed x1, local copies, waits for them, and re-layouts  2.21 us

profile of v1, /device:TPU:0, one launch (start us, length us, event | category | flops | bytes accessed | tf_op | source)
XLA Modules:
  0.0 65.2 jit_solution(7123535245849220509)
XLA Ops:
  0.6 0.8 %compare_select_fusion = s32[2,14]{1,0:T(2,128)S(1)} fusion(s32[2,14]{1,0:T(2,128)} %param.9, s32[2,14]{1,0:T(2,128)} %param.10, s32[]{:T(128)S(6)} %mul.7, s32[2]{0:T(128)} %param.11), kind=kLoop, calls=%fused_computation.2 | loop fusion | flops 168 | bytes 348 | tf_op jit(solution)/shard_map/jit(_where)/select_n | solution.py:392
  1.4 0.1 copy.11
  1.5 0.1 fusion
  1.6 0.6 reshape.11.w_ref
  2.2 58.4 %shard_map.103 = (f32[2,2,480,128]{3,2,1,0:T(8,128)}, f32[2,8,128]{2,1,0:T(8,128)}) custom-call(f32[96]{0:T(128)} %reshape.11.w_ref, s32[2,128]{1,0:T(2,128)} %stype.1, f32[8,2,480,128]{3,2,1,0:T(8,128)} %basis.1, f32[8,480,480]{2,1,0:T(8,128)} %trans.1, f32[8,128,128]{2,1,0:T(8,128)} %coup.1, f32[4,480,480]{2,1,0:T(8,128)} %tmat.1), custom_call_target="tpu_custom_call" | custom-call | tf_op jit(solution)/shard_map/pallas_call | solution.py:403
  60.6 1.2 %slice_bitcast_fusion = f32[10]{0:T(128)} fusion(f32[2,8,128]{2,1,0:T(8,128)} %get-tuple-element.6), kind=kLoop, calls=%fused_computation.3 | loop fusion | bytes 80 | tf_op jit(solution)/shard_map/squeeze | solution.py:446
  61.8 1.2 %slice_bitcast_fusion.1 = f32[9]{0:T(128)} fusion(f32[2,8,128]{2,1,0:T(8,128)} %get-tuple-element.6), kind=kLoop, calls=%fused_computation.4 | loop fusion | bytes 72 | tf_op jit(solution)/shard_map/squeeze | solution.py:446
  63.0 2.2 %copy.13 = f32[2,2,480,128]{3,2,1,0:T(8,128)} copy(f32[2,2,480,128]{3,2,1,0:T(8,128)} %get-tuple-element.10) | data formatting | bytes 1966080
